TPU v7x, 32 devices: a whole 2x2x4 slice. The times are simulated.
32 devices in a mesh: groups: 2 (over y), tm: 4 (over z), chan: 4 (over x, core).
Axes of the slice: x: 2, y: 2, z: 4, core: 2. Of those that a mesh axis runs over, the one named last changes fastest.
Arguments:
- vis: bfloat16 [8, 128, 2, 128], P(('groups', 'chan'), 'tm'), parts along dimension 0, may hold values from -6 to 6
- row_weight: bfloat16 [8, 128, 128, 128], P(('groups', 'chan'), 'tm'), parts along dimension 0, may hold values from -4 to 4
- col_weight: bfloat16 [8, 128, 128, 256], P(('groups', 'chan'), 'tm'), parts along dimension 0, may hold values from -0.5 to 0.5
- w_bin: int32 [8, 128, 1], P(('groups', 'chan'), 'tm'), parts along dimension 0, may hold values from 0 to 3; in each aligned block of 32 rows (0 to 31, 32 to 63, ..., all dimensions but the last counted through in order) at most 16 rows name the same one
- tile_col: int32 [8, 128], P(('groups', 'chan'), 'tm'), parts along dimension 0, may hold values from 0 to 15
- w_kernel: bfloat16 [8, 512, 512], P(('groups', 'tm')), parts along dimension 0, may hold values from -0.25 to 0.25
Outputs:
- grid: float32 [8, 128, 16, 512], P(('groups', 'tm'), 'chan'), parts along dimension 0
There are 2 independent parts, one for each index of `groups`. A program takes and returns all parts, laid end to end along the dimension named above; each array names one. Nothing has to cross between parts.
Inputs may be any that keep to these rules, and one draw needn't show every extreme that they name: `w_bin`: within the blocks of one device (aligned blocks of 32 along the channel-group and block dimensions taken together), no w-plane is named more than 16 times, a bound that some block reaches.
All inputs are finite; a program needn't handle non-finite values.
Results may differ from a plain program's by a relative error of at most 0.0041.
Values may be sent and summed in bfloat16 or wider, within the bound.
A program may use at most 128 MiB of HBM per device.

v0:
```python
import jax
import jax.numpy as jnp
from jax import lax
from jax.sharding import PartitionSpec as P

QW = 256
GC = 4096


def grid_group(total, weighted, columns, targets):
    patch = jnp.einsum("ghkv,gvq->gkhq", weighted, columns, preferred_element_type=jnp.float32)
    flat = patch.reshape(patch.shape[0], -1)
    return total.at[targets].add(flat, mode="drop")


def weigh_rows(rows, visibility):
    return (
        rows.astype(jnp.float32)[:, None, :, :] * visibility.astype(jnp.float32)[:, :, None, :]
    ).astype(jnp.bfloat16)


def body(vis, row_weight, col_weight, w_bin, tile_col, w_kernel):
    planes = lax.axis_size("tm")
    count = vis.shape[1]
    rows_k = row_weight.shape[2]
    width_v = vis.shape[3]
    width_q = col_weight.shape[3]
    tile_count = GC // QW
    per_plane = 2 * count // planes
    slot_total = planes * per_plane
    turns = 4
    group_len = slot_total // turns
    bins = w_bin[0, :, 0]
    tiles = tile_col[0]
    member = (bins[:, None] == jnp.arange(planes, dtype=jnp.int32)[None, :]).astype(jnp.int32)
    before = jnp.cumsum(member, axis=0) - member
    within = jnp.sum(before * member, axis=1)
    target = bins * per_plane + within
    source = (
        jnp.full((slot_total,), count, jnp.int32).at[target].set(jnp.arange(count, dtype=jnp.int32))
    )
    filled = source < count
    picked = jnp.minimum(source, count - 1)
    slot_tile = jnp.where(filled, tiles[picked], tile_count).reshape(planes, per_plane)
    columns = jnp.take(col_weight[0], picked, axis=0).reshape(planes, per_plane, width_v, width_q)
    start = jnp.zeros((tile_count, rows_k * 2 * width_q), jnp.float32)
    rows_sent = jnp.take(row_weight[0], picked, axis=0).reshape(planes, per_plane, rows_k, width_v)
    vis_sent = jnp.take(vis[0], picked, axis=0).reshape(planes, per_plane, 2, width_v)
    got_rows, got_vis, got_columns, got_tiles = (
        lax.all_to_all(rows_sent, "tm", split_axis=0, concat_axis=0, tiled=True),
        lax.all_to_all(vis_sent, "tm", split_axis=0, concat_axis=0, tiled=True),
        lax.all_to_all(columns, "tm", split_axis=0, concat_axis=0, tiled=True),
        lax.all_to_all(slot_tile, "tm", split_axis=0, concat_axis=0, tiled=True),
    )

    def step_raw(total, group):
        rows, visibility, cols, targets = group
        return (grid_group(total, weigh_rows(rows, visibility), cols, targets), None)

    groups = (
        got_rows.reshape(turns, group_len, rows_k, width_v),
        got_vis.reshape(turns, group_len, 2, width_v),
        got_columns.reshape(turns, group_len, width_v, width_q),
        got_tiles.reshape(turns, group_len),
    )
    total, _ = lax.scan(step_raw, start, groups)
    partial_value = total.reshape(tile_count, rows_k, 2 * width_q)
    share = rows_k // lax.axis_size("chan")
    summed = lax.psum(partial_value, "chan")
    mine = lax.dynamic_slice_in_dim(summed, lax.axis_index("chan") * share, share, 1)
    rounded = mine.astype(jnp.bfloat16)
    result = jnp.einsum("tkq,qr->ktr", rounded, w_kernel[0], preferred_element_type=jnp.float32)
    return result[None]


def solution(mesh):
    in_specs = (
        P(("groups", "chan"), "tm", None, None),
        P(("groups", "chan"), "tm", None, None),
        P(("groups", "chan"), "tm", None, None),
        P(("groups", "chan"), "tm", None),
        P(("groups", "chan"), "tm"),
        P(("groups", "tm"), None, None),
    )
    out_specs = P(("groups", "tm"), "chan", None, None)
    return jax.shard_map(body, mesh=mesh, in_specs=in_specs, out_specs=out_specs, check_vma=False)
```

profile of v0, /device:TPU:0, one launch (start us, length us, event | category | flops | bytes accessed | tf_op | source)
XLA Modules:
  0.0 493.3 jit_solution(4983551968529737838)
XLA Ops:
  0.0 0.0 copy-start
  0.0 0.9 fusion.8
  0.9 0.1 reduce_window_sum.11
  0.9 0.8 select_reduce_fusion
  1.8 0.7 fusion.9
  2.4 0.7 scatter_custom_fusion.1
  3.1 1.4 gather_fusion
  4.6 0.7 all_to_all.17
  5.3 6.3 %all-to-all-start = ((s32[4,1,16]{2,1,0:T(1,128)}), s32[4,1,16]{2,1,0:T(1,128)S(1)}, u32[]{:S(2)}, u32[]{:S(2)}) async-start(s32[4,1,16]{2,1,0:T(1,128)} %bitcast.13), calls=%async_computation | async-start | bytes 4096 | tf_op jit(solution)/shard_map/all_to_all | solution.py:53
  11.6 0.1 broadcast_in_dim.53
  11.7 1.4 gather_fusion.3
  13.1 0.8 broadcast_select_fusion.2
  13.8 3.4 gather_fusion.2
  17.2 0.0 all-to-all-done
  17.2 5.1 %all-to-all-start.3 = ((bf16[4,16,2,128]{3,2,1,0:T(2,128)(2,1)}), bf16[4,16,2,128]{3,2,1,0:T(2,128)(2,1)S(1)}, u32[]{:S(2)}, u32[]{:S(2)}) async-start(bf16[4,16,2,128]{3,2,1,0:T(2,128)(2,1)} %broadcast_select_fusion.2), calls=%async_computation.3 | async-start | bytes 65536 | tf_op jit(solution)/shard_map/all_to_all | solution.py:51
  22.3 3.2 broadcast_select_fusion.1
  25.6 2.4 all-to-all-done.3
  28.0 4.4 all-to-all-start.2
  32.4 0.0 copy-done
  32.4 2.8 gather_fusion.1
  35.2 6.4 %copy.14 = bf16[64,128,256]{1,2,0:T(8,128)(2,1)} copy(bf16[64,128,256]{2,1,0:T(8,128)(2,1)} %gather_fusion.1) | data formatting | bytes 8388608 | tf_op jit(solution)/shard_map/jit(_take)/gather | solution.py:45
  41.6 4.6 broadcast_select_fusion
  46.2 32.8 %all-to-all-done.2 = bf16[4,16,128,128]{3,2,1,0:T(8,128)(2,1)} async-done(((bf16[4,16,128,128]{3,2,1,0:T(8,128)(2,1)}), bf16[4,16,128,128]{3,2,1,0:T(8,128)(2,1)}, u32[]{:S(2)}, u32[]{:S(2)}) %all-to-all-start.2) | async-done | bytes 2097184 | tf_op jit(solution)/shard_map/all_to_all | solution.py:50
  79.0 5.0 %all-to-all-start.1 = ((bf16[4,16,128,256]{2,3,1,0:T(8,128)(2,1)}), bf16[4,16,128,256]{2,3,1,0:T(8,128)(2,1)}, u32[]{:S(2)}, u32[]{:S(2)}) async-start(bf16[4,16,128,256]{2,3,1,0:T(8,128)(2,1)} %broadcast_select_fusion), calls=%async_computation.1 | async-start | bytes 8388608 | tf_op jit(solution)/shard_map/all_to_all | solution.py:52
  84.0 92.6 %all-to-all-done.1 = bf16[4,16,128,256]{2,3,1,0:T(8,128)(2,1)} async-done(((bf16[4,16,128,256]{2,3,1,0:T(8,128)(2,1)}), bf16[4,16,128,256]{2,3,1,0:T(8,128)(2,1)}, u32[]{:S(2)}, u32[]{:S(2)}) %all-to-all-start.1) | async-done | bytes 4194336 | tf_op jit(solution)/shard_map/all_to_all | solution.py:52
  176.6 2.2 broadcast_in_dim.50
  178.8 228.1 %while.10 = (s32[]{:T(128)}, f32[16,65536]{1,0:T(8,128)}, s32[4,16]{1,0:T(4,128)S(1)}, bf16[4,16,128,256]{2,3,1,0:T(8,128)(2,1)}, bf16[4,16,128,128]{3,2,1,0:T(8...) while((s32[]{:T(128)}, f32[16,65536]{1,0:T(8,128)}, s32[4,16]{1,0:T(4,128)S(1)}, ...), condition=%wide.region_5.6_spmd, body=%wide.region_3.5_spmd.sunk | while | flops 270798912 | bytes 37266200 | solution.py:66
  178.8 1.1 bitcast_convert_fusion.5
  180.0 3.9 convolution_bitcast_fusion.3
  183.9 7.2 %copy.19 = f32[16,128,2,256]{3,2,1,0:T(2,128)} copy(f32[16,128,2,256]{1,3,2,0:T(8,128)} %convolution_bitcast_fusion.3) | data formatting | bytes 8388608 | tf_op jit(solution)/shard_map/while/body/eval_jaxpr/ghkv,gvq->gkhq/transpose | solution.py:11
  191.1 6.3 %reshape.160 = f32[16,65536]{1,0:T(8,128)} reshape(f32[16,128,2,256]{3,2,1,0:T(2,128)} %copy.19) | data formatting | bytes 8388608 | tf_op jit(solution)/shard_map/while/body/eval_jaxpr/reshape | solution.py:12
  197.4 38.6 %scatter_fusion = f32[16,65536]{1,0:T(8,128)} fusion(f32[16,65536]{1,0:T(8,128)} %get-tuple-element.97, s32[16]{0:T(128)S(1)} %fusion.16, f32[16,65536]{1,0:T(8,128)} %reshape.160), kind=kCustom, calls=%fused_computation.4.clone.1 | custom fusion | flops 1048576 | bytes 12582976 | tf_op jit(solution)/shard_map/while/body/eval_jaxpr/scatter-add | solution.py:13
  236.0 1.1 bitcast_convert_fusion.5
  237.2 3.9 convolution_bitcast_fusion.3
  241.1 7.2 %copy.19 = f32[16,128,2,256]{3,2,1,0:T(2,128)} copy(f32[16,128,2,256]{1,3,2,0:T(8,128)} %convolution_bitcast_fusion.3) | data formatting | bytes 8388608 | tf_op jit(solution)/shard_map/while/body/eval_jaxpr/ghkv,gvq->gkhq/transpose | solution.py:11
  248.3 6.3 %reshape.160 = f32[16,65536]{1,0:T(8,128)} reshape(f32[16,128,2,256]{3,2,1,0:T(2,128)} %copy.19) | data formatting | bytes 8388608 | tf_op jit(solution)/shard_map/while/body/eval_jaxpr/reshape | solution.py:12
  254.6 38.5 %scatter_fusion = f32[16,65536]{1,0:T(8,128)} fusion(f32[16,65536]{1,0:T(8,128)} %get-tuple-element.97, s32[16]{0:T(128)S(1)} %fusion.16, f32[16,65536]{1,0:T(8,128)} %reshape.160), kind=kCustom, calls=%fused_computation.4.clone.1 | custom fusion | flops 1048576 | bytes 12582976 | tf_op jit(solution)/shard_map/while/body/eval_jaxpr/scatter-add | solution.py:13
  293.1 1.1 bitcast_convert_fusion.5
  294.3 3.9 convolution_bitcast_fusion.3
  298.2 7.2 %copy.19 = f32[16,128,2,256]{3,2,1,0:T(2,128)} copy(f32[16,128,2,256]{1,3,2,0:T(8,128)} %convolution_bitcast_fusion.3) | data formatting | bytes 8388608 | tf_op jit(solution)/shard_map/while/body/eval_jaxpr/ghkv,gvq->gkhq/transpose | solution.py:11
  305.4 6.3 %reshape.160 = f32[16,65536]{1,0:T(8,128)} reshape(f32[16,128,2,256]{3,2,1,0:T(2,128)} %copy.19) | data formatting | bytes 8388608 | tf_op jit(solution)/shard_map/while/body/eval_jaxpr/reshape | solution.py:12
  311.7 38.1 %scatter_fusion = f32[16,65536]{1,0:T(8,128)} fusion(f32[16,65536]{1,0:T(8,128)} %get-tuple-element.97, s32[16]{0:T(128)S(1)} %fusion.16, f32[16,65536]{1,0:T(8,128)} %reshape.160), kind=kCustom, calls=%fused_computation.4.clone.1 | custom fusion | flops 1048576 | bytes 12582976 | tf_op jit(solution)/shard_map/while/body/eval_jaxpr/scatter-add | solution.py:13
  349.8 1.1 bitcast_convert_fusion.5
  351.0 3.9 convolution_bitcast_fusion.3
  354.9 7.2 %copy.19 = f32[16,128,2,256]{3,2,1,0:T(2,128)} copy(f32[16,128,2,256]{1,3,2,0:T(8,128)} %convolution_bitcast_fusion.3) | data formatting | bytes 8388608 | tf_op jit(solution)/shard_map/while/body/eval_jaxpr/ghkv,gvq->gkhq/transpose | solution.py:11
  362.1 6.3 %reshape.160 = f32[16,65536]{1,0:T(8,128)} reshape(f32[16,128,2,256]{3,2,1,0:T(2,128)} %copy.19) | data formatting | bytes 8388608 | tf_op jit(solution)/shard_map/while/body/eval_jaxpr/reshape | solution.py:12
  368.4 38.5 %scatter_fusion = f32[16,65536]{1,0:T(8,128)} fusion(f32[16,65536]{1,0:T(8,128)} %get-tuple-element.97, s32[16]{0:T(128)S(1)} %fusion.16, f32[16,65536]{1,0:T(8,128)} %reshape.160), kind=kCustom, calls=%fused_computation.4.clone.1 | custom fusion | flops 1048576 | bytes 12582976 | tf_op jit(solution)/shard_map/while/body/eval_jaxpr/scatter-add | solution.py:13
  406.9 6.5 %copy.17 = f32[2,8,128,512]{3,2,1,0:T(8,128)} copy(f32[2,8,128,512]{3,1,2,0:T(8,128)} %bitcast.63) | data formatting | bytes 8388608
  413.5 0.0 copy-start.1
  413.5 76.7 %all-reduce.1 = bf16[16,128,512]{2,1,0:T(8,128)(2,1)} all-reduce(f32[16,128,512]{2,1,0:T(8,128)} %bitcast.66), channel_id=1, replica_groups=mesh['groups'=2,'tm'=4,'chan'=4] {'chan'}, use_global_device_ids=true, to_apply=%region_6.7 | all-reduce | flops 1048576 | bytes 6291456 | tf_op jit(solution)/shard_map/psum | solution.py:69
  490.2 0.0 copy-done.1
  490.2 1.5 convolution_bitcast_fusion.1
  491.7 1.6 copy.15
  (12 shorter events, 0.1 us)
Async XLA Ops:
  0.0 32.4 %copy-start = (bf16[1,32,128,256]{3,2,1,0:T(8,128)(2,1)S(1)}, bf16[1,32,128,256]{3,2,1,0:T(8,128)(2,1)}, u32[]{:S(2)}) copy-start(bf16[1,32,128,256]{3,2,1,0:T(8,128)(2,1)} %param.10) | copy-start | bytes 6291460
  5.3 11.9 %all-to-all-start = ((s32[4,1,16]{2,1,0:T(1,128)}), s32[4,1,16]{2,1,0:T(1,128)S(1)}, u32[]{:S(2)}, u32[]{:S(2)}) async-start(s32[4,1,16]{2,1,0:T(1,128)} %bitcast.13), calls=%async_computation | async-start | bytes 4096 | tf_op jit(solution)/shard_map/all_to_all | solution.py:53
  17.2 10.7 %all-to-all-start.3 = ((bf16[4,16,2,128]{3,2,1,0:T(2,128)(2,1)}), bf16[4,16,2,128]{3,2,1,0:T(2,128)(2,1)S(1)}, u32[]{:S(2)}, u32[]{:S(2)}) async-start(bf16[4,16,2,128]{3,2,1,0:T(2,128)(2,1)} %broadcast_select_fusion.2), calls=%async_computation.3 | async-start | bytes 65536 | tf_op jit(solution)/shard_map/all_to_all | solution.py:51
  28.0 51.0 %all-to-all-start.2 = ((bf16[4,16,128,128]{3,2,1,0:T(8,128)(2,1)}), bf16[4,16,128,128]{3,2,1,0:T(8,128)(2,1)}, u32[]{:S(2)}, u32[]{:S(2)}) async-start(bf16[4,16,128,128]{3,2,1,0:T(8,128)(2,1)} %broadcast_select_fusion.1), calls=%async_computation.2 | async-start | bytes 4194304 | tf_op jit(solution)/shard_map/all_to_all | solution.py:50
  79.0 97.6 %all-to-all-start.1 = ((bf16[4,16,128,256]{2,3,1,0:T(8,128)(2,1)}), bf16[4,16,128,256]{2,3,1,0:T(8,128)(2,1)}, u32[]{:S(2)}, u32[]{:S(2)}) async-start(bf16[4,16,128,256]{2,3,1,0:T(8,128)(2,1)} %broadcast_select_fusion), calls=%async_computation.1 | async-start | bytes 8388608 | tf_op jit(solution)/shard_map/all_to_all | solution.py:52
  413.5 76.7 %copy-start.1 = (bf16[1,512,512]{2,1,0:T(8,128)(2,1)S(1)}, bf16[1,512,512]{2,1,0:T(8,128)(2,1)}, u32[]{:S(2)}) copy-start(bf16[1,512,512]{2,1,0:T(8,128)(2,1)} %param.13) | copy-start | bytes 1572868
where the time goes:
time: 493 us
  other arithmetic  169 us (34%)
  waiting for transfers between devices  128 us (26%)
  local copies, waits for them, and re-layouts  81.2 us (16%)
  blocking collectives  76.7 us (16%)
  starting transfers between devices  20.9 us (4%)
  matrix products  17.1 us (3%)
    scatter-add x4, other arithmetic, grid_group(): return total.at[targets].add(flat, mode='drop')  154 us
    all_to_all x1, waiting for transfers between devices, body(): lax.all_to_all(columns, 'tm', split_axis=0, concat_axis=0, tiled=True)  92.6 us
    psum x1, blocking collectives, body(): summed = lax.psum(partial_value, 'chan')  76.7 us
    all_to_all x1, waiting for transfers between devices, body(): lax.all_to_all(rows_sent, 'tm', split_axis=0, concat_axis=0, tiled=True)  32.8 us
    transpose x4, local copies, waits for them, and re-layouts, grid_group(): jnp.einsum('ghkv,gvq->gkhq', weighted, columns, preferred_element_type=jn...  28.8 us
    reshape x4, local copies, waits for them, and re-layouts, grid_group(): flat = patch.reshape(patch.shape[0], -1)  25.2 us
    dot_general x4, matrix products, grid_group(): jnp.einsum('ghkv,gvq->gkhq', weighted, columns, preferred_element_type=jn...  15.7 us
  transfers between devices with their start and end apart: 4, of which 3 were waited for; matrix products, arithmetic and copies ran while one was open for 5% of the time, Pallas kernels for 0%

commit v1 on v0

v1 whole, which is shorter than its diff:
```python
import functools
import jax
import jax.numpy as jnp
from jax import lax
from jax.experimental import pallas as pl
from jax.experimental.pallas import tpu as pltpu
from jax.sharding import PartitionSpec as P

QW = 256
GC = 4096
MESH = pl.DeviceIdType.MESH
LIMIT = 60 * 1024 * 1024


def pair_of(me):
    return me + 1 - 2 * (me % 2)


def swap_kernel(vis, rows, cols, seg, vis_p, rows_p, cols_p, seg_p, send, recv):
    me = lax.axis_index("chan")
    other = pair_of(me)
    barrier = pltpu.get_barrier_semaphore()
    pl.semaphore_signal(barrier, inc=1, device_id={"chan": other}, device_id_type=MESH)
    pl.semaphore_wait(barrier, 1)
    moves = ((seg, seg_p), (vis, vis_p), (rows.at[:, :, other % 2], rows_p), (cols, cols_p))
    copies = [
        pltpu.make_async_remote_copy(
            src_ref=src, dst_ref=dst, send_sem=send.at[i], recv_sem=recv.at[i],
            device_id={"chan": other}, device_id_type=MESH,
        )
        for i, (src, dst) in enumerate(moves)
    ]
    for copy in copies:
        copy.start()
    for copy in copies:
        copy.wait()


def swap(vis, rows, cols, seg):
    any_spec = pl.BlockSpec(memory_space=pl.ANY)
    count, fold, _, share, width = rows.shape
    shapes = (
        jax.ShapeDtypeStruct(vis.shape, vis.dtype),
        jax.ShapeDtypeStruct((count, fold, share, width), rows.dtype),
        jax.ShapeDtypeStruct(cols.shape, cols.dtype),
        jax.ShapeDtypeStruct(seg.shape, seg.dtype),
    )
    return pl.pallas_call(
        swap_kernel,
        out_shape=shapes,
        in_specs=[any_spec] * 4,
        out_specs=[any_spec] * 4,
        scratch_shapes=[pltpu.SemaphoreType.DMA((4,)), pltpu.SemaphoreType.DMA((4,))],
        compiler_params=pltpu.CompilerParams(collective_id=0, has_side_effects=True),
        name="swap",
    )(vis, rows, cols, seg)


def patch_kernel(cells, batch, seg_o, seg_p, half, vis_o, rows_o, cols_o, vis_p, rows_p, cols_p, out, acc):
    g, s = pl.program_id(0), pl.program_id(1)
    fold, share = out.shape[0], out.shape[2]
    span = fold * share

    @pl.when(s == 0)
    def _():
        def clear(c, carry):
            acc[c] = jnp.zeros(acc.shape[1:], acc.dtype)
            return carry
        lax.fori_loop(0, cells, clear, 0)

    for seg, vis, rows, cols in ((seg_o, vis_o, rows_o, cols_o), (seg_p, vis_p, rows_p, cols_p)):
        for i in range(batch):
            cell = seg[s * batch + i] - g * cells

            @pl.when((cell >= 0) & (cell < cells))
            def _():
                block = rows[i].reshape(span, rows.shape[-1])
                weighted = jnp.concatenate([block * vis[i, 0:1, :], block * vis[i, 1:2, :]], axis=0)
                patch = jnp.dot(weighted, cols[i], preferred_element_type=jnp.float32)
                acc[cell, :, 0:QW] += patch[:span]
                acc[cell, :, QW:2 * QW] += patch[span:]

    @pl.when(s == pl.num_programs(1) - 1)
    def _():
        def put(c, carry):
            for x in range(fold):
                out[x, c] = acc[c, x * share:(x + 1) * share, :].astype(out.dtype)
            return carry
        lax.fori_loop(0, cells, put, 0)


def patches(planes, tiles, seg_o, seg_p, half, vis_o, rows_o, cols_o, vis_p, rows_p, cols_p):
    count, fold, _, share, width = rows_o.shape
    together = 4 if planes % 4 == 0 else 1
    cells = together * tiles
    batch = 4 if count % 4 == 0 else 1
    wide = cols_o.shape[2]
    vis_spec = pl.BlockSpec((batch, 2, width), lambda g, s, a, b, h: (s, 0, 0))
    cols_spec = pl.BlockSpec((batch, width, wide), lambda g, s, a, b, h: (s, 0, 0))
    rows_own = pl.BlockSpec((batch, fold, None, share, width), lambda g, s, a, b, h: (s, 0, h[0], 0, 0))
    rows_got = pl.BlockSpec((batch, fold, share, width), lambda g, s, a, b, h: (s, 0, 0, 0))
    return pl.pallas_call(
        functools.partial(patch_kernel, cells, batch),
        out_shape=jax.ShapeDtypeStruct((fold, planes * tiles, share, 2 * wide), jnp.bfloat16),
        grid_spec=pltpu.PrefetchScalarGridSpec(
            num_scalar_prefetch=3,
            grid=(planes // together, count // batch),
            in_specs=[vis_spec, rows_own, cols_spec, vis_spec, rows_got, cols_spec],
            out_specs=pl.BlockSpec((fold, cells, share, 2 * wide), lambda g, s, a, b, h: (0, g, 0, 0)),
            scratch_shapes=[pltpu.VMEM((cells, fold * share, 2 * wide), jnp.float32)],
        ),
        compiler_params=pltpu.CompilerParams(
            dimension_semantics=("arbitrary", "arbitrary"), vmem_limit_bytes=LIMIT
        ),
        name="patches",
    )(seg_o, seg_p, half, vis_o, rows_o, cols_o, vis_p, rows_p, cols_p)


def reduce_kernel(planes, fold, turns, part, kern, out, own, xgot, zgot, lsem, xsend, xrecv, zsend, zrecv):
    me, mine = lax.axis_index("chan"), lax.axis_index("tm")
    core, row = me % 2, me // 2
    size = own.shape[1] // turns

    def x_peer(d):
        return {"chan": ((row + d) % fold) * 2 + core}

    def z_peer(d):
        return {"tm": (mine + d) % planes}

    barrier = pltpu.get_barrier_semaphore()
    for d in range(1, fold):
        pl.semaphore_signal(barrier, inc=1, device_id=x_peer(d), device_id_type=MESH)

    def hail(d, carry):
        pl.semaphore_signal(barrier, inc=1, device_id=z_peer(d), device_id_type=MESH)
        return carry
    lax.fori_loop(1, planes, hail, 0)
    pl.semaphore_wait(barrier, fold + planes - 2)

    def x_copy(j, d):
        cut = pl.ds(j * size, size)
        return pltpu.make_async_remote_copy(
            src_ref=part.at[(row + d) % fold, :, cut], dst_ref=xgot.at[d - 1, :, cut],
            send_sem=xsend.at[j, d - 1], recv_sem=xrecv.at[j, d - 1],
            device_id=x_peer(d), device_id_type=MESH,
        )

    def z_copy(j, d):
        cut = pl.ds(j * size, size)
        return pltpu.make_async_remote_copy(
            src_ref=own.at[(mine + d) % planes, cut], dst_ref=zgot.at[d - 1, cut],
            send_sem=zsend.at[j, d - 1], recv_sem=zrecv.at[j, d - 1],
            device_id=z_peer(d), device_id_type=MESH,
        )

    def l_copy(j):
        cut = pl.ds(j * size, size)
        return pltpu.make_async_copy(part.at[row, :, cut], own.at[:, cut], lsem.at[j])

    for j in range(turns):
        for d in range(1, fold):
            x_copy(j, d).start()
        l_copy(j).start()

    def over_x(w, t):
        total = own[w, t].astype(jnp.float32)
        for d in range(1, fold):
            total = total + xgot[d - 1, w, t].astype(jnp.float32)
        return total

    for j in range(turns):
        l_copy(j).wait()
        for d in range(1, fold):
            x_copy(j, d).wait_recv()

        def forward(d, carry):
            w = (mine + d) % planes
            for t in range(j * size, (j + 1) * size):
                own[w, t] = over_x(w, t).astype(own.dtype)
            z_copy(j, d).start()
            return carry
        lax.fori_loop(1, planes, forward, 0)

    share, wide = own.shape[2], own.shape[3]
    for j in range(turns):
        def arrive(d, carry):
            z_copy(j, d).wait_recv()
            return carry
        lax.fori_loop(1, planes, arrive, 0)
        for t in range(j * size, (j + 1) * size):
            def add(d, total):
                return total + zgot[d - 1, t].astype(jnp.float32)
            total = lax.fori_loop(1, planes, add, over_x(mine, t), unroll=planes <= 4)
            out[t] = jnp.dot(total.astype(jnp.bfloat16), kern[...], preferred_element_type=jnp.float32)

    for j in range(turns):
        for d in range(1, fold):
            x_copy(j, d).wait_send()

        def leave(d, carry):
            z_copy(j, d).wait_send()
            return carry
        lax.fori_loop(1, planes, leave, 0)


def reduce_grids(part, kern, planes, turns):
    fold, _, tiles, share, wide = part.shape
    return pl.pallas_call(
        functools.partial(reduce_kernel, planes, fold, turns),
        out_shape=jax.ShapeDtypeStruct((tiles, share, wide), jnp.float32),
        in_specs=[pl.BlockSpec(memory_space=pl.ANY), pl.BlockSpec(memory_space=pltpu.VMEM)],
        out_specs=pl.BlockSpec(memory_space=pltpu.VMEM),
        scratch_shapes=[
            pltpu.VMEM((planes, tiles, share, wide), jnp.bfloat16),
            pltpu.VMEM((fold - 1, planes, tiles, share, wide), jnp.bfloat16),
            pltpu.VMEM((planes - 1, tiles, share, wide), jnp.bfloat16),
            pltpu.SemaphoreType.DMA((turns,)),
            pltpu.SemaphoreType.DMA((turns, fold - 1)),
            pltpu.SemaphoreType.DMA((turns, fold - 1)),
            pltpu.SemaphoreType.DMA((turns, planes - 1)),
            pltpu.SemaphoreType.DMA((turns, planes - 1)),
        ],
        compiler_params=pltpu.CompilerParams(
            collective_id=1, has_side_effects=True, vmem_limit_bytes=LIMIT
        ),
        name="reduce_grids",
    )(part, kern)


def body(vis, row_weight, col_weight, w_bin, tile_col, w_kernel):
    planes = lax.axis_size("tm")
    chans = lax.axis_size("chan")
    count, rows_k, width_v = row_weight.shape[1:]
    tile_count = GC // QW
    share = rows_k // chans
    fold = chans // 2
    seg = w_bin[0, :, 0] * tile_count + tile_col[0]
    held = jnp.zeros((8, 128), jnp.int32).at[0, :count].set(seg)
    rows = row_weight[0].reshape(count, fold, 2, share, width_v)
    vis_p, rows_p, cols_p, held_p = swap(vis[0], rows, col_weight[0], held)
    half = (lax.axis_index("chan") % 2).reshape(1).astype(jnp.int32)
    part = patches(
        planes, tile_count, seg, held_p[0, :count], half,
        vis[0], rows, col_weight[0], vis_p, rows_p, cols_p,
    )
    part = part.reshape(fold, planes, tile_count, share, part.shape[-1])
    result = reduce_grids(part, w_kernel[0], planes, 4)
    return jnp.transpose(result, (1, 0, 2))[None]


def solution(mesh):
    in_specs = (
        P(("groups", "chan"), "tm", None, None),
        P(("groups", "chan"), "tm", None, None),
        P(("groups", "chan"), "tm", None, None),
        P(("groups", "chan"), "tm", None),
        P(("groups", "chan"), "tm"),
        P(("groups", "tm"), None, None),
    )
    out_specs = P(("groups", "tm"), "chan", None, None)
    return jax.shard_map(body, mesh=mesh, in_specs=in_specs, out_specs=out_specs, check_vma=False)
```

time: 493 us -> 92.4 us (0.19)
  other arithmetic: 169 us -> 1.92 us
  waiting for transfers between devices: 128 us -> 0 us
  Pallas kernels: 0 us -> 85 us
  blocking collectives: 76.7 us -> 0 us
  local copies, waits for them, and re-layouts: 81.2 us -> 4.58 us
  starting transfers between devices: 20.9 us -> 0 us
  matrix products: 17.1 us -> 0 us
    scatter-add x4 -> x0, other arithmetic: 154 us -> none  [grid_group(): return total.at[targets].add(flat, mode='drop')]
    all_to_all x4 -> x0, waiting for transfers between devices: 128 us -> none  [the longest x1 92.6 us: body(): lax.all_to_all(columns, 'tm', split_axis=0, concat_axis=0, tiled=True)]
    pallas_call x0 -> x3, Pallas kernels: none -> 85 us  [the longest x1 64.5 us: reduce_grids(): pl.pallas_call(functools.partial(reduce_kernel, planes, fold, turns), out...]
    psum x1 -> x0, blocking collectives: 76.7 us -> none  [body(): summed = lax.psum(partial_value, 'chan')]
    transpose x4 -> x0, local copies, waits for them, and re-layouts: 28.8 us -> none  [grid_group(): jnp.einsum('ghkv,gvq->gkhq', weighted, columns, preferred_element_type=jn...]
    reshape x4 -> x0, local copies, waits for them, and re-layouts: 25.2 us -> none  [grid_group(): flat = patch.reshape(patch.shape[0], -1)]
    all_to_all x4 -> x0, starting transfers between devices: 20.9 us -> none  [the longest x1 6.35 us: body(): lax.all_to_all(slot_tile, 'tm', split_axis=0, concat_axis=0, tiled=True)]
    dot_general x5 -> x0, matrix products: 17.1 us -> none  [the longest x4 15.7 us: grid_group(): jnp.einsum('ghkv,gvq->gkhq', weighted, columns, preferred_element_type=jn...]
  transfers between devices with their start and end apart: 4 -> 0, of which waited for: 3 -> 0; matrix products, arithmetic and copies ran while one was open for 5% -> 0% of each run, Pallas kernels for 0% -> 0%
where the time goes in v1:
time: 92.4 us; the launch traced here: 91.6 us
  Pallas kernels  85 us (92%)
  local copies, waits for them, and re-layouts  4.58 us (5%)
  other arithmetic  1.92 us (2%)
    pallas_call x1, Pallas kernels, reduce_grids(): pl.pallas_call(functools.partial(reduce_kernel, planes, fold, turns), out...  64.5 us
    pallas_call x1, Pallas kernels, patches(): pl.pallas_call(functools.partial(patch_kernel, cells, batch), out_shape=j...  15.1 us
    pallas_call x1, Pallas kernels, swap(): pl.pallas_call(swap_kernel, out_shape=shapes, in_specs=[any_spec] * 4, ou...  5.47 us
    broadcast_in_dim x1, local copies, waits for them, and re-layouts, body(): return jnp.transpose(result, (1, 0, 2))[None]  2.81 us
    add x2, other arithmetic, body(): seg = w_bin[0, :, 0] * tile_count + tile_col[0]  1.92 us

profile of v1, /device:TPU:0, one launch (start us, length us, event | category | flops | bytes accessed | tf_op | source)
XLA Modules:
  0.0 91.6 jit_solution(5711861259888437635)
XLA Ops:
  0.0 0.7 bitcast_add_fusion
  0.7 1.2 %bitcast_add_fusion.1.seg_o = s32[32]{0:T(128)} fusion(s32[1,32]{1,0:T(1,128)} %param.12, s32[1,32,1]{1,2,0:T(1,128)} %param.11), kind=kLoop, calls=%fused_computation.1 | loop fusion | flops 64 | bytes 384 | tf_op jit(solution)/shard_map/add | solution.py:237
  1.9 0.6 scatter.4.seg
  2.5 5.5 %swap.1 = (bf16[32,2,128]{2,1,0:T(2,128)(2,1)}, bf16[32,2,32,128]{3,2,1,0:T(8,128)(2,1)}, bf16[32,128,256]{2,1,0:T(8,128)(2,1)}, s32[8,128]{1,0:T(8,128)}) custom-call(bf16[32,2,128]{2,1,0:T(2,128)(2,1)} %bitcast.24, bf16[32,2,2,32,128]{4,3,2,1,0:T(8,128)(2,1)} %bitcast.21, bf16[32,128,256]{2,1,0:T(8,128)(2,1)} %bitcast.18, s32[8,128]{1,0:T(8,128)} %scatter.4.seg), custom_call_target="tpu_custom_call" | custom-call | tf_op jit(solution)/shard_map/swap/pallas_call | solution.py:48
  8.0 1.2 %slice_bitcast_fusion.seg_p = s32[32]{0:T(128)} fusion(s32[8,128]{1,0:T(8,128)} %get-tuple-element.21), kind=kLoop, calls=%fused_computation.2 | loop fusion | bytes 256 | tf_op jit(solution)/shard_map/squeeze | solution.py:243
  9.2 15.1 %patches.1 = bf16[2,64,32,512]{3,2,1,0:T(8,128)(2,1)} custom-call(s32[32]{0:T(128)} %bitcast_add_fusion.1.seg_o, s32[32]{0:T(128)} %slice_bitcast_fusion.seg_p, s32[1]{0:T(128)} %bitcast.7.half, bf16[32,2,128]{2,1,0:T(2,128)(2,1)} %bitcast.25, bf16[32,2,2,32,128]{4,3,2,1,0:T(8,128)(2,1)} %bitcast.22, bf16[32,128,256]{2,1,0:T(8,128)(2,1)} %bitcast.19, ...), custom_call_target="tpu_custom_call" | custom-call | tf_op jit(solution)/shard_map/patches/pallas_call | solution.py:102
  24.3 64.5 %reduce_grids.1 = f32[16,32,512]{2,1,0:T(8,128)} custom-call(bf16[2,4,16,32,512]{4,3,2,1,0:T(8,128)(2,1)} %bitcast.17, bf16[512,512]{1,0:T(8,128)(2,1)} %bitcast.23), custom_call_target="tpu_custom_call" | custom-call | tf_op jit(solution)/shard_map/reduce_grids/pallas_call | solution.py:208
  88.8 2.8 %copy.7 = f32[1,32,16,512]{3,2,1,0:T(8,128)} copy(f32[1,32,16,512]{3,1,2,0:T(8,128)} %bitcast.20) | data formatting | bytes 2097152 | tf_op jit(solution)/shard_map/broadcast_in_dim | solution.py:248

commit v2 on v0

v2 whole, which is shorter than its diff:
```python
import functools
import jax
import jax.numpy as jnp
from jax import lax
from jax.experimental import pallas as pl
from jax.experimental.pallas import tpu as pltpu
from jax.sharding import PartitionSpec as P

QW = 256
GC = 4096
MESH = pl.DeviceIdType.MESH
LIMIT = 63 * 1024 * 1024
TURNS = 8


def pair_of(me):
    return me + 1 - 2 * (me % 2)


def exchange_kernel(
    planes, tiles, turns, table, vis, rows, cols, kern, out,
    tab_s, tab_v, vis_v, rows_v, cols_v, kern_v, runs, xout, xgot, zgot,
    lsem, ssend, srecv, xsend, xrecv, zsend, zrecv,
):
    me, mine = lax.axis_index("chan"), lax.axis_index("tm")
    core, row = me % 2, me // 2
    other = pair_of(me)
    count, fold, share = rows_v.shape[1], rows_v.shape[2], rows_v.shape[3]
    size = tiles // turns

    def x_peer(d):
        return {"chan": ((row + d) % fold) * 2 + core}

    def z_peer(d):
        return {"tm": (mine + d) % planes}

    local = [
        pltpu.make_async_copy(src, dst, lsem.at[i])
        for i, (src, dst) in enumerate((
            (table, tab_s.at[0]), (vis, vis_v.at[0]), (rows.at[:, :, core], rows_v.at[0]),
            (cols, cols_v.at[0]), (kern, kern_v),
        ))
    ]
    for copy in local:
        copy.start()

    barrier = pltpu.get_barrier_semaphore()
    pl.semaphore_signal(barrier, inc=1, device_id={"chan": other}, device_id_type=MESH)
    for d in range(1, fold):
        pl.semaphore_signal(barrier, inc=1, device_id=x_peer(d), device_id_type=MESH)

    def hail(d, carry):
        pl.semaphore_signal(barrier, inc=1, device_id=z_peer(d), device_id_type=MESH)
        return carry
    lax.fori_loop(1, planes, hail, 0)
    pl.semaphore_wait(barrier, fold + planes - 1)

    swaps = [
        pltpu.make_async_remote_copy(
            src_ref=src, dst_ref=dst, send_sem=ssend.at[i], recv_sem=srecv.at[i],
            device_id={"chan": other}, device_id_type=MESH,
        )
        for i, (src, dst) in enumerate((
            (table, tab_v), (vis, vis_v.at[1]), (rows.at[:, :, other % 2], rows_v.at[1]),
            (cols, cols_v.at[1]),
        ))
    ]
    for copy in swaps:
        copy.start()

    for s in range(2):
        runs[s, 0] = jnp.zeros(runs.shape[2:], runs.dtype)

    def entry(s, i):
        return tab_s[s, i // 128, i % 128]

    batch = 4 if count % 4 == 0 else 1

    def build(s, x):
        def step(i, carry):
            found = []
            for u in range(batch):
                b = i * batch + u
                block = rows_v[s, b, x]
                weighted = jnp.concatenate(
                    [block * vis_v[s, b, 0:1, :], block * vis_v[s, b, 1:2, :]], axis=0
                )
                found.append(jnp.dot(weighted, cols_v[s, b], preferred_element_type=jnp.float32))
            for u in range(batch):
                b = i * batch + u
                last = entry(s, b)
                runs[s, b + 1, :, 0:QW] = found[u][:share] + runs[s, last, :, 0:QW]
                runs[s, b + 1, :, QW:2 * QW] = found[u][share:] + runs[s, last, :, QW:2 * QW]
            return carry
        lax.fori_loop(0, count // batch, step, 0)

    def cell(w, t):
        i = count + w * tiles + t
        return runs[0, entry(0, i)] + runs[1, entry(1, i)]

    def x_copy(j, d):
        cut = pl.ds(j * size, size)
        return pltpu.make_async_remote_copy(
            src_ref=xout.at[d - 1, :, cut], dst_ref=xgot.at[d - 1, :, cut],
            send_sem=xsend.at[j, d - 1], recv_sem=xrecv.at[j, d - 1],
            device_id=x_peer(d), device_id_type=MESH,
        )

    def z_copy(j, d):
        cut = pl.ds(j * size, size)
        return pltpu.make_async_remote_copy(
            src_ref=xgot.at[0, (mine + d) % planes, cut], dst_ref=zgot.at[d - 1, cut],
            send_sem=zsend.at[j, d - 1], recv_sem=zrecv.at[j, d - 1],
            device_id=z_peer(d), device_id_type=MESH,
        )

    for copy in local[:4]:
        copy.wait()
    for d in range(1, fold):
        half = (row + d) % fold
        build(0, half)
        if d == 1:
            for copy in swaps:
                copy.wait_recv()
            last_copy = pltpu.make_async_copy(tab_v, tab_s.at[1], lsem.at[5])
            last_copy.start()
            last_copy.wait()
        build(1, half)
        for j in range(turns):
            def fill(w, carry):
                for t in range(j * size, (j + 1) * size):
                    xout[d - 1, w, t] = cell(w, t).astype(xout.dtype)
                return carry
            lax.fori_loop(0, planes, fill, 0)
            x_copy(j, d).start()
    build(0, row)
    build(1, row)

    def over_x(w, t):
        total = cell(w, t)
        for d in range(1, fold):
            total = total + xgot[d - 1, w, t].astype(jnp.float32)
        return total

    def finish(j):
        def arrive(d, carry):
            z_copy(j, d).wait_recv()
            return carry
        lax.fori_loop(1, planes, arrive, 0)
        for t in range(j * size, (j + 1) * size):
            def add(d, total):
                return total + zgot[d - 1, t].astype(jnp.float32)
            total = lax.fori_loop(1, planes, add, over_x(mine, t), unroll=planes <= 4)
            out[t] = jnp.dot(total.astype(jnp.bfloat16), kern_v[...], preferred_element_type=jnp.float32)

    local[4].wait()
    for j in range(turns):
        for d in range(1, fold):
            x_copy(j, d).wait_recv()

        def forward(d, carry):
            w = (mine + d) % planes
            for t in range(j * size, (j + 1) * size):
                xgot[0, w, t] = over_x(w, t).astype(xgot.dtype)
            z_copy(j, d).start()
            return carry
        lax.fori_loop(1, planes, forward, 0)

    for j in range(turns):
        finish(j)

    for copy in swaps:
        copy.wait_send()
    for j in range(turns):
        for d in range(1, fold):
            x_copy(j, d).wait_send()

        def leave(d, carry):
            z_copy(j, d).wait_send()
            return carry
        lax.fori_loop(1, planes, leave, 0)


def exchange(table, vis, rows, cols, kern, planes, tiles, turns):
    count, fold, _, share, width = rows.shape
    wide = 2 * cols.shape[2]
    any_spec = pl.BlockSpec(memory_space=pl.ANY)
    half = jnp.bfloat16
    dma = pltpu.SemaphoreType.DMA
    return pl.pallas_call(
        functools.partial(exchange_kernel, planes, tiles, turns),
        out_shape=jax.ShapeDtypeStruct((tiles, share, wide), jnp.float32),
        in_specs=[any_spec] * 5,
        out_specs=pl.BlockSpec(memory_space=pltpu.VMEM),
        scratch_shapes=[
            pltpu.SMEM((2,) + table.shape, jnp.int32),
            pltpu.VMEM(table.shape, jnp.int32),
            pltpu.VMEM((2,) + vis.shape, vis.dtype),
            pltpu.VMEM((2, count, fold, share, width), rows.dtype),
            pltpu.VMEM((2,) + cols.shape, cols.dtype),
            pltpu.VMEM(kern.shape, kern.dtype),
            pltpu.VMEM((2, count + 1, share, wide), jnp.float32),
            pltpu.VMEM((fold - 1, planes, tiles, share, wide), half),
            pltpu.VMEM((fold - 1, planes, tiles, share, wide), half),
            pltpu.VMEM((planes - 1, tiles, share, wide), half),
            dma((6,)),
            dma((4,)),
            dma((4,)),
            dma((turns, fold - 1)),
            dma((turns, fold - 1)),
            dma((turns, planes - 1)),
            dma((turns, planes - 1)),
        ],
        compiler_params=pltpu.CompilerParams(
            collective_id=0, has_side_effects=True, vmem_limit_bytes=LIMIT
        ),
        name="exchange",
    )(table, vis, rows, cols, kern)


def links(seg, cells):
    count = seg.shape[0]
    place = jnp.arange(count, dtype=jnp.int32)
    same = (seg[:, None] == seg[None, :]) & (place[None, :] < place[:, None])
    before = jnp.max(jnp.where(same, place[None, :] + 1, 0), axis=1)
    named = seg[None, :] == jnp.arange(cells, dtype=jnp.int32)[:, None]
    final = jnp.max(jnp.where(named, place[None, :] + 1, 0), axis=1)
    both = jnp.concatenate([before, final])
    return jnp.pad(both, (0, -both.shape[0] % 1024)).reshape(-1, 128)


def body(vis, row_weight, col_weight, w_bin, tile_col, w_kernel):
    planes = lax.axis_size("tm")
    chans = lax.axis_size("chan")
    count, rows_k, width_v = row_weight.shape[1:]
    tile_count = GC // QW
    fold = chans // 2
    table = links(w_bin[0, :, 0] * tile_count + tile_col[0], planes * tile_count)
    rows = row_weight[0].reshape(count, fold, 2, rows_k // chans, width_v)
    result = exchange(table, vis[0], rows, col_weight[0], w_kernel[0], planes, tile_count, TURNS)
    return jnp.transpose(result, (1, 0, 2))[None]


def solution(mesh):
    in_specs = (
        P(("groups", "chan"), "tm", None, None),
        P(("groups", "chan"), "tm", None, None),
        P(("groups", "chan"), "tm", None, None),
        P(("groups", "chan"), "tm", None),
        P(("groups", "chan"), "tm"),
        P(("groups", "tm"), None, None),
    )
    out_specs = P(("groups", "tm"), "chan", None, None)
    return jax.shard_map(body, mesh=mesh, in_specs=in_specs, out_specs=out_specs, check_vma=False)
```

time: 493 us -> 72.9 us (0.15)
  other arithmetic: 169 us -> 1.7 us
  waiting for transfers between devices: 128 us -> 0 us
  local copies, waits for them, and re-layouts: 81.2 us -> 3.41 us
  blocking collectives: 76.7 us -> 0 us
  Pallas kernels: 0 us -> 67.6 us
  starting transfers between devices: 20.9 us -> 0 us
  matrix products: 17.1 us -> 0 us
    scatter-add x4 -> x0, other arithmetic: 154 us -> none  [grid_group(): return total.at[targets].add(flat, mode='drop')]
    all_to_all x4 -> x0, waiting for transfers between devices: 128 us -> none  [the longest x1 92.6 us: body(): lax.all_to_all(columns, 'tm', split_axis=0, concat_axis=0, tiled=True)]
    psum x1 -> x0, blocking collectives: 76.7 us -> none  [body(): summed = lax.psum(partial_value, 'chan')]
    pallas_call x0 -> x1, Pallas kernels: none -> 67.6 us  [exchange(): pl.pallas_call(functools.partial(exchange_kernel, planes, tiles, turns),...]
    transpose x4 -> x0, local copies, waits for them, and re-layouts: 28.8 us -> none  [grid_group(): jnp.einsum('ghkv,gvq->gkhq', weighted, columns, preferred_element_type=jn...]
    reshape x4 -> x1, local copies, waits for them, and re-layouts: 25.2 us -> 0.6 us  [links(): return jnp.pad(both, (0, -both.shape[0] % 1024)).reshape(-1, 128)]
    all_to_all x4 -> x0, starting transfers between devices: 20.9 us -> none  [the longest x1 6.35 us: body(): lax.all_to_all(slot_tile, 'tm', split_axis=0, concat_axis=0, tiled=True)]
    dot_general x5 -> x0, matrix products: 17.1 us -> none  [the longest x4 15.7 us: grid_group(): jnp.einsum('ghkv,gvq->gkhq', weighted, columns, preferred_element_type=jn...]
  transfers between devices with their start and end apart: 4 -> 0, of which waited for: 3 -> 0; matrix products, arithmetic and copies ran while one was open for 5% -> 0% of each run, Pallas kernels for 0% -> 0%
where the time goes in v2:
time: 72.9 us; the launch traced here: 72.7 us
  Pallas kernels  67.6 us (93%)
  local copies, waits for them, and re-layouts  3.41 us (5%)
  other arithmetic  1.7 us (2%)
    pallas_call x1, Pallas kernels, exchange(): pl.pallas_call(functools.partial(exchange_kernel, planes, tiles, turns),...  67.6 us
    broadcast_in_dim x1, local copies, waits for them, and re-layouts, body(): return jnp.transpose(result, (1, 0, 2))[None]  2.81 us

profile of v2, /device:TPU:0, one launch (start us, length us, event | category | flops | bytes accessed | tf_op | source)
XLA Modules:
  0.0 72.7 jit_solution(6288124771360068919)
XLA Ops:
  0.0 0.7 fusion.1
  0.7 0.7 bitcast_add_fusion.1
  1.4 0.2 select_reduce_fusion.1
  1.5 0.1 select_reduce_fusion
  1.6 0.1 pad_add_fusion
  1.7 0.6 pad_bitcast_fusion.table
  2.3 67.6 %exchange.1 = f32[16,32,512]{2,1,0:T(8,128)} custom-call(s32[8,128]{1,0:T(8,128)} %pad_bitcast_fusion.table, bf16[32,2,128]{2,1,0:T(2,128)(2,1)} %bitcast.23, bf16[32,2,2,32,128]{4,3,2,1,0:T(8,128)(2,1)} %bitcast.21, bf16[32,128,256]{2,1,0:T(8,128)(2,1)} %bitcast.20, bf16[512,512]{1,0:T(8,128)(2,1)} %bitcast.22), custom_call_target="tpu_custom_call" | custom-call | tf_op jit(solution)/shard_map/exchange/pallas_call | solution.py:190
  69.9 2.8 %copy.8 = f32[1,32,16,512]{3,2,1,0:T(8,128)} copy(f32[1,32,16,512]{3,1,2,0:T(8,128)} %bitcast.19) | data formatting | bytes 2097152 | tf_op jit(solution)/shard_map/broadcast_in_dim | solution.py:241
